TPU v7x, 32 devices: a whole 2x2x4 slice. The times are simulated.
32 devices in a mesh: row: 8 (over y, x, core), col: 4 (over z).
Axes of the slice: x: 2, y: 2, z: 4, core: 2. Of those that a mesh axis runs over, the one named last changes fastest.
Arguments:
- species: float32 [2, 256, 256, 128], P(None, None, 'row', 'col'), may hold values from -6 to 6
- coupling: float32 [2, 2], replicated, may hold values from -4 to 4
- symbol_x: float32 [256], replicated, may hold values from 0.3 to 3
- symbol_y: float32 [256], replicated, may hold values from 0.3 to 3
- symbol_z: float32 [128], replicated, may hold values from 0.3 to 3
Outputs:
- modes: float32 [2, 256, 256, 128], P(None, 'row', 'col')
All inputs are finite; a program needn't handle non-finite values.
Results may differ from a plain program's by a relative error of at most 0.000078.
Values sent between devices are 32-bit elements.
No kernel may reach another device: no remote copies, remote signals or barrier semaphores. Data moves between devices by JAX's collectives and lax.ppermute only.
A program may use at most 128 MiB of HBM per device.

v0:
```python
import functools

import jax
import jax.numpy as jnp
import numpy as np
from jax import lax
from jax.experimental import pallas as pl
from jax.experimental.pallas import tpu as pltpu
from jax.sharding import PartitionSpec as P


LANES = 128
SPARE = 4 << 20
SHARES = (1, 2, 3, 2)


ANY = pl.BlockSpec(memory_space=pl.ANY)
VMEM = pl.BlockSpec(memory_space=pltpu.VMEM)
HBM = pl.BlockSpec(memory_space=pltpu.HBM)
SMEM = pl.BlockSpec(memory_space=pltpu.SMEM)


def mode_table(count):
    rank = np.arange(1, count + 1)
    angle = np.pi / (count + 1) * (rank[:, None] * rank[None, :] % (2 * count + 2))
    return np.sin(angle) * np.sqrt(2.0 / (count + 1))


def split_table(table):
    table = table.astype(np.float32)
    high = table.astype(jnp.bfloat16)
    low = (table - high.astype(np.float32)).astype(jnp.bfloat16)
    return high, low


def split(values):
    high = values.astype(jnp.bfloat16)
    low = (values - high.astype(jnp.float32)).astype(jnp.bfloat16)
    return high, low


def dot(a, b, contract):
    return lax.dot_general(
        a, b, ((contract[:1], contract[1:]), ((), ())), preferred_element_type=jnp.float32
    )


def block_transpose(tiles, width):
    count = len(tiles)
    lane = lax.broadcasted_iota(jnp.int32, tiles[0].shape, 1)
    step = count // 2
    while step:
        odd = (lane // (width * step)) % 2 == 1
        result = list(tiles)
        for g in range(count):
            if g & step:
                continue
            a, b = tiles[g], tiles[g + step]
            shift = width * step
            result[g] = jnp.where(odd, pltpu.roll(b, shift, 1), a)
            result[g + step] = jnp.where(odd, b, pltpu.roll(a, LANES - shift, 1))
        tiles = result
        step //= 2
    return tiles


def x_kernel(chips, units, groups, first, lines, table_ref, *refs):
    if not first:
        refs = refs[len(units) * chips :]
    outs, refs = refs[: len(units) * chips], refs[len(units) * chips :]
    scratch = refs[0]
    fields, rows, _ = lines.shape
    blocks = rows // LANES
    share_y = blocks * groups
    me = lax.axis_index("row")
    pair = me % 2
    owner = pair if first else 1 - pair
    if first:
        source, sems = refs[1:]
        loads = [
            pltpu.make_async_copy(lines.at[f], source.at[f], sems.at[f]) for f in range(fields)
        ]
        for load in loads:
            load.start()
    else:
        source = lines
    depth = table_ref.shape[0] // 2
    table = table_ref[pl.ds(pl.multiple_of(pair * depth, depth), depth), :]
    half = depth // 2
    tall = scratch.shape[2] // blocks
    for f in range(fields):
        if first:
            loads[f].wait()
        high, low = split(source[f])
        both = dot(table, high, (1, 1))
        result = both[:half] + both[half:] + dot(table[:half], low, (1, 1))
        for j in range(half // tall):
            for b in range(blocks):
                scratch[f, j, b * tall : (b + 1) * tall, :] = result[
                    j * tall : (j + 1) * tall, b * LANES : (b + 1) * LANES
                ]
        start = 0
        for q, count in enumerate(units):
            for k in range(chips):
                chip = (me // 2) ^ k
                for hi in range(count):
                    tiles = []
                    for g in range(groups):
                        at = (start + hi * groups + g) * chips
                        place = pl.ds(at % tall + chip, blocks, stride=tall)
                        tiles.append(scratch[f, at // tall, place, :])
                    for t, tile in enumerate(block_transpose(tiles, LANES // groups)):
                        place = pl.ds(
                            pl.multiple_of(owner * share_y + t * blocks, blocks), blocks
                        )
                        outs[q * chips + k][f, place, hi * LANES : (hi + 1) * LANES] = tile
            start += count * groups


def y_kernel(peers, heads, *refs):
    ins, refs = refs[:peers], refs[peers:]
    table, outs, gathered = refs[0], refs[1 : 1 + heads], refs[1 + heads]
    fields, share = ins[0].shape[:2]
    out_share = outs[0].shape[1]
    chip, col = lax.axis_index("row") // 2, lax.axis_index("col")
    left = jnp.concatenate(
        [
            table[pl.ds(pl.multiple_of((col ^ k) * out_share, out_share), out_share), :]
            for k in range(heads)
        ],
        axis=0,
    )
    for f in range(fields):
        for k in range(peers):
            place = pl.ds(pl.multiple_of((chip ^ k) * share, share), share)
            high, low = split(ins[k][f])
            gathered[f, 0, place, :] = high
            gathered[f, 1, place, :] = low
    for f in range(fields):
        high, low = gathered[f, 0], gathered[f, 1]
        result = dot(left, jnp.concatenate([high, high, low], axis=0), (1, 0))
        for k in range(heads):
            outs[k][f] = result[k * out_share : (k + 1) * out_share]


def z_table_kernel(peers, groups, table_high, table_low, wide):
    depth, out_width = table_high.shape
    z_share = depth // peers
    col = lax.axis_index("col")
    wide[...] = jnp.zeros_like(wide)
    for part, table in enumerate((table_high, table_low, table_high)):
        for k in range(peers):
            piece = table[pl.ds(pl.multiple_of((col ^ k) * z_share, z_share), z_share), :]
            for g in range(groups):
                start = (part * peers + k) * LANES + g * z_share
                wide[start : start + z_share, g * out_width : (g + 1) * out_width] = piece


def z_kernel(peers, groups, first, has_prior, *refs):
    ins, refs = refs[:peers], refs[peers:]
    wide, syz, symbol_x, coupling = refs[:4]
    modes, mixed, sems = refs[4 + has_prior :]
    fields, share, lanes = ins[0].shape
    units = lanes // LANES
    out_width = wide.shape[1] // groups
    row = lax.axis_index("row")
    parts = []
    for hi in range(units):
        for f in range(fields):
            block = jnp.concatenate(
                [ins[k][f, :, hi * LANES : (hi + 1) * LANES] for k in range(peers)], axis=1
            )
            high, low = split(block)
            parts.append(jnp.concatenate([high, high, low], axis=1))
    old = dot(jnp.concatenate(parts, axis=0), wide[...], (1, 0))
    stores = []
    for hi in range(units):
        for g in range(groups):
            kx = hi * groups + g
            line = row * (symbol_x.shape[0] // lax.axis_size("row")) + first + kx
            weight = 1.0 / (syz[...] + symbol_x[line])
            rest = 1.0 - weight
            mine = [
                old[
                    (hi * fields + f) * share : (hi * fields + f + 1) * share,
                    g * out_width : (g + 1) * out_width,
                ]
                for f in range(fields)
            ]
            for a in range(fields):
                mix = coupling[a, 0] * mine[0]
                for b in range(1, fields):
                    mix = mix + coupling[a, b] * mine[b]
                mixed[a, kx] = weight * mine[a] + rest * mix
        stores.append(
            pltpu.make_async_copy(
                mixed.at[:, hi * groups : (hi + 1) * groups],
                modes.at[:, pl.ds(first + hi * groups, groups)],
                sems.at[hi],
            )
        )
        stores[-1].start()
    for store in stores:
        store.wait()


def solution(mesh):
    rows, cols = mesh.shape["row"], mesh.shape["col"]
    n_chunk = len(SHARES)

    def exchange(arrays, axis):
        count = mesh.shape[axis]
        step = count // len(arrays)
        moved = [arrays[0]]
        for k in range(1, len(arrays)):
            pairs = [(i, i ^ (k * step)) for i in range(count)]
            moved.append(lax.ppermute(arrays[k], axis, pairs))
        return moved

    def local(species, coupling, symbol_x, symbol_y, symbol_z):
        fields, size_x, share_y, share_z = species.shape
        size_y, size_z = share_y * rows, share_z * cols
        share_kx, share_ky = size_x // rows, size_y // cols
        groups = LANES // share_z
        blocks = share_y // groups
        all_units = share_kx // groups
        units = [all_units * s // sum(SHARES) for s in SHARES]
        assert sum(units) == all_units
        firsts = [groups * sum(units[:q]) for q in range(n_chunk)]
        f32, bf16 = jnp.float32, jnp.bfloat16

        def limit(*shapes):
            total = sum(int(np.prod(shape)) * size for shape, size in shapes)
            return pltpu.CompilerParams(vmem_limit_bytes=total + SPARE)

        def cost(flops, moved):
            return pl.CostEstimate(flops=flops, bytes_accessed=moved, transcendentals=0)

        lines = jnp.transpose(species, (0, 2, 3, 1)).reshape(fields, share_y * share_z, size_x)

        chips = rows // 2
        tall = max(chips, 8)
        tables_x = []
        for pair in range(2):
            picked = [
                (chip * 2 + pair) * share_kx + kx for kx in range(share_kx) for chip in range(chips)
            ]
            tables_x += split_table(mode_table(size_x)[picked])
        table_x = jnp.asarray(np.concatenate(tables_x, axis=0))
        message_shapes = [
            jax.ShapeDtypeStruct((fields, 2 * share_y, u * LANES), f32)
            for u in units
            for _ in range(chips)
        ]

        def x_step(values, sent):
            own = sent is None
            sent = sent or []
            return pl.pallas_call(
                functools.partial(x_kernel, chips, units, groups, own),
                out_shape=message_shapes,
                in_specs=[HBM if own else VMEM, VMEM] + [VMEM] * len(sent),
                out_specs=[VMEM] * len(message_shapes),
                input_output_aliases={2 + i: i for i in range(len(sent))},
                scratch_shapes=[
                    pltpu.VMEM(
                        (fields, share_kx * chips // tall, blocks * tall, LANES), f32
                    )
                ]
                + [
                    pltpu.VMEM(lines.shape, f32),
                    pltpu.SemaphoreType.DMA((fields,)),
                ]
                * own,
                cost_estimate=cost(3 * lines.size * size_x, 8 * lines.size),
                compiler_params=limit((lines.shape, 24)),
                name="x_step",
            )(values, table_x, *sent)

        other = lax.ppermute(lines, "row", [(i, i ^ 1) for i in range(rows)])
        sent = x_step(other, x_step(lines, None))

        order = [
            peer * share_y + b * groups + t
            for peer in range(rows)
            for t in range(groups)
            for b in range(blocks)
        ]
        high, low = split_table(mode_table(size_y)[:, order])
        table_y = jnp.asarray(np.concatenate([high, low, high], axis=1))

        def y_step(arrays):
            lanes = arrays[0].shape[2]
            shape = jax.ShapeDtypeStruct((fields, share_ky, lanes), f32)
            return pl.pallas_call(
                functools.partial(y_kernel, chips, cols),
                out_shape=[shape] * cols,
                in_specs=[VMEM] * (chips + 1),
                out_specs=[VMEM] * cols,
                scratch_shapes=[pltpu.VMEM((fields, 2, size_y, lanes), bf16)],
                cost_estimate=cost(
                    6 * fields * size_y * size_y * lanes, 8 * fields * size_y * lanes
                ),
                compiler_params=limit(((fields, size_y, lanes), 24), (table_y.shape, 4)),
                name="y_step",
            )(*arrays, table_y)

        table_z = [jnp.asarray(t) for t in split_table(mode_table(size_z))]
        wide_shape = (3 * cols * LANES, groups * size_z)
        wide = pl.pallas_call(
            functools.partial(z_table_kernel, cols, groups),
            out_shape=jax.ShapeDtypeStruct(wide_shape, bf16),
            in_specs=[VMEM] * 2,
            out_specs=VMEM,
            compiler_params=limit((wide_shape, 2)),
            cost_estimate=cost(2 * size_z**3, 2 * int(np.prod(wide_shape))),
            name="z_table",
        )(*table_z)
        part_y = lax.dynamic_slice_in_dim(symbol_y, lax.axis_index("col") * share_ky, share_ky)
        syz = 1.0 + (part_y[:, None] + symbol_z[None, :])
        out_shape = jax.ShapeDtypeStruct((fields, share_kx, share_ky, size_z), f32)

        def z_step(q, arrays, prior):
            lanes = arrays[0].shape[2]
            has_prior = prior is not None
            return pl.pallas_call(
                functools.partial(z_kernel, cols, groups, firsts[q], has_prior),
                out_shape=out_shape,
                in_specs=[VMEM] * (cols + 2) + [SMEM] * 2 + [ANY] * has_prior,
                out_specs=ANY,
                input_output_aliases={cols + 4: 0} if has_prior else {},
                scratch_shapes=[
                    pltpu.VMEM((fields, units[q] * groups, share_ky, size_z), f32),
                    pltpu.SemaphoreType.DMA((units[q],)),
                ],
                cost_estimate=cost(
                    6 * fields * share_ky * lanes * cols * groups * size_z,
                    8 * cols * fields * share_ky * lanes,
                ),
                compiler_params=limit(
                    ((cols, fields, share_ky, lanes), 24), (wide_shape, 4)
                ),
                name="z_step",
            )(*arrays, wide, syz, symbol_x, coupling, *([prior] if has_prior else []))

        lines_z = []
        for q in range(n_chunk):
            received = exchange(sent[q * chips : (q + 1) * chips], "row")
            lines_z.append(exchange(y_step(received), "col"))
        modes = None
        for q in range(n_chunk):
            modes = z_step(q, lines_z[q], modes)
        return modes

    return jax.shard_map(
        local,
        mesh=mesh,
        in_specs=(P(None, None, "row", "col"), P(), P(), P(), P()),
        out_specs=P(None, "row", "col", None),
        check_vma=False,
    )
```

profile of v0, /device:TPU:16, one launch (start us, length us, event | category | flops | bytes accessed | tf_op | source)
XLA Modules:
  0.0 90.0 jit_solution(15411360666356573936)
XLA Ops:
  0.0 1.6 %copy-done.1 = f32[2,256,32,32]{1,3,2,0:T(8,128)S(1)} copy-done((f32[2,256,32,32]{1,3,2,0:T(8,128)S(1)}, f32[2,256,32,32]{1,3,2,0:T(8,128)}, u32[]{:S(2)}) %copy-start.1) | copy-done | bytes 2097176
  1.6 0.9 %copy-done.2 = bf16[512,256]{1,0:T(8,128)(2,1)S(1)} copy-done((bf16[512,256]{1,0:T(8,128)(2,1)S(1)}, bf16[512,256]{1,0:T(8,128)(2,1)}, u32[]{:S(2)}) %copy-start.2) | copy-done | bytes 262168
  2.5 1.8 %x_step.2 = (f32[2,64,128]{2,1,0:T(8,128)S(1)}, f32[2,64,128]{2,1,0:T(8,128)S(1)}, f32[2,64,128]{2,1,0:T(8,128)S(1)}, f32[2,64,128]{2,1,0:T(8,128)S(1)}, f32[2,6...) custom-call(f32[2,1024,256]{2,1,0:T(8,128)S(1)} %bitcast.4, ...), custom_call_target="tpu_custom_call" | custom-call | flops 402653184 | bytes 4194304 | tf_op jit(solution)/shard_map/x_step/pallas_call | solution.py:259
  4.3 0.1 collective-permute-done.lines
  4.4 1.1 %x_step.3 = (f32[2,64,128]{2,1,0:T(8,128)S(1)}, f32[2,64,128]{2,1,0:T(8,128)S(1)}, f32[2,64,128]{2,1,0:T(8,128)S(1)}, f32[2,64,128]{2,1,0:T(8,128)S(1)}, f32[2,6...) custom-call(f32[2,1024,256]{2,1,0:T(8,128)S(1)} %collective-permute-, ...), custom_call_target="tpu_custom_call", output_to_operand_aliasing={{0}: (2, {}), {1}: (3, {}), {2}: (4, {}), {3}: (5, {}), {4}... | custom-call | flops 402653184 | bytes 4194304 | tf_op jit(solution)/shard_map/x_step/pallas_call | solution.py:259
  5.5 0.0 copy-start.4
  5.6 0.0 copy-start.5
  5.6 1.6 %collective-permute-start.19 = (f32[2,64,128]{2,1,0:T(8,128)S(1)}, f32[2,64,128]{2,1,0:T(8,128)S(1)}, u32[]{:S(2)}, u32[]{:S(2)}) collective-permute-start(f32[2,64,128]{2,1,0:T(8,128)S(1)} %get-tuple-element.94), channel_id=1, source_target_pairs={{0,8},{4,12},{8,0},{12,4},{16,24},{20,28},{24,16},{28,20},{1,9},{5... | collective-permute-start | bytes 196616 | tf_op jit(solution)/shard_map/ppermute | solution.py:217
  7.1 1.5 %collective-permute-start.20 = (f32[2,64,128]{2,1,0:T(8,128)S(1)}, f32[2,64,128]{2,1,0:T(8,128)S(1)}, u32[]{:S(2)}, u32[]{:S(2)}) collective-permute-start(f32[2,64,128]{2,1,0:T(8,128)S(1)} %get-tuple-element.95), channel_id=1, source_target_pairs={{0,16},{4,20},{8,24},{12,28},{16,0},{20,4},{24,8},{28,12},{1,17},{... | collective-permute-start | bytes 196616 | tf_op jit(solution)/shard_map/ppermute | solution.py:217
  8.6 0.5 collective-permute-start.21
  9.1 1.5 %collective-permute-start.7 = (f32[2,64,384]{2,1,0:T(8,128)S(1)}, f32[2,64,384]{2,1,0:T(8,128)S(1)}, u32[]{:S(2)}, u32[]{:S(2)}) collective-permute-start(f32[2,64,384]{2,1,0:T(8,128)S(1)} %get-tuple-element.78), channel_id=1, source_target_pairs={{0,8},{4,12},{8,0},{12,4},{16,24},{20,28},{24,16},{28,20},{1,9},{5... | collective-permute-start | bytes 589832 | tf_op jit(solution)/shard_map/ppermute | solution.py:217
  10.6 1.5 %collective-permute-start.8 = (f32[2,64,384]{2,1,0:T(8,128)S(1)}, f32[2,64,384]{2,1,0:T(8,128)S(1)}, u32[]{:S(2)}, u32[]{:S(2)}) collective-permute-start(f32[2,64,384]{2,1,0:T(8,128)S(1)} %get-tuple-element.79), channel_id=1, source_target_pairs={{0,16},{4,20},{8,24},{12,28},{16,0},{20,4},{24,8},{28,12},{1,17},{... | collective-permute-start | bytes 589832 | tf_op jit(solution)/shard_map/ppermute | solution.py:217
  12.1 0.5 collective-permute-start.1
  12.7 1.4 %collective-permute-start.9 = (f32[2,64,384]{2,1,0:T(8,128)S(1)}, f32[2,64,384]{2,1,0:T(8,128)S(1)}, u32[]{:S(2)}, u32[]{:S(2)}) collective-permute-start(f32[2,64,384]{2,1,0:T(8,128)S(1)} %get-tuple-element.80), channel_id=1, source_target_pairs={{0,24},{4,28},{8,16},{12,20},{16,8},{20,12},{24,0},{28,4},{1,25},{... | collective-permute-start | bytes 589832 | tf_op jit(solution)/shard_map/ppermute | solution.py:217
  14.1 0.4 collective-permute-done.21.refs_3_
  14.5 0.6 collective-permute-start.13
  15.1 5.5 %collective-permute-done.1.refs_1_ = f32[2,64,256]{2,1,0:T(8,128)S(1)} collective-permute-done((f32[2,64,256]{2,1,0:T(8,128)S(1)}, f32[2,64,256]{2,1,0:T(8,128)S(1)}, u32[]{:S(2)}, u32[]{:S(2)}) %collective-permute-start.1) | collective-permute-done | bytes 131104 | tf_op jit(solution)/shard_map/ppermute | solution.py:217
  20.6 1.5 %collective-permute-start.14 = (f32[2,64,256]{2,1,0:T(8,128)S(1)}, f32[2,64,256]{2,1,0:T(8,128)S(1)}, u32[]{:S(2)}, u32[]{:S(2)}) collective-permute-start(f32[2,64,256]{2,1,0:T(8,128)S(1)} %get-tuple-element.87), channel_id=1, source_target_pairs={{0,16},{4,20},{8,24},{12,28},{16,0},{20,4},{24,8},{28,12},{1,17},{... | collective-permute-start | bytes 393224 | tf_op jit(solution)/shard_map/ppermute | solution.py:217
  22.1 4.5 %collective-permute-done.13.refs_1_ = f32[2,64,256]{2,1,0:T(8,128)S(1)} collective-permute-done((f32[2,64,256]{2,1,0:T(8,128)S(1)}, f32[2,64,256]{2,1,0:T(8,128)S(1)}, u32[]{:S(2)}, u32[]{:S(2)}) %collective-permute-start.13) | collective-permute-done | bytes 131104 | tf_op jit(solution)/shard_map/ppermute | solution.py:217
  26.6 1.9 %collective-permute-start.15 = (f32[2,64,256]{2,1,0:T(8,128)S(1)}, f32[2,64,256]{2,1,0:T(8,128)S(1)}, u32[]{:S(2)}, u32[]{:S(2)}) collective-permute-start(f32[2,64,256]{2,1,0:T(8,128)S(1)} %get-tuple-element.88), channel_id=1, source_target_pairs={{0,24},{4,28},{8,16},{12,20},{16,8},{20,12},{24,0},{28,4},{1,25},{... | collective-permute-start | bytes 393224 | tf_op jit(solution)/shard_map/ppermute | solution.py:217
  28.4 0.5 collective-permute-start.2
  28.9 2.2 %collective-permute-start.3 = (f32[2,64,256]{2,1,0:T(8,128)S(1)}, f32[2,64,256]{2,1,0:T(8,128)S(1)}, u32[]{:S(2)}, u32[]{:S(2)}) collective-permute-start(f32[2,64,256]{2,1,0:T(8,128)S(1)} %get-tuple-element.72), channel_id=1, source_target_pairs={{0,24},{4,28},{8,16},{12,20},{16,8},{20,12},{24,0},{28,4},{1,25},{... | collective-permute-start | bytes 393224 | tf_op jit(solution)/shard_map/ppermute | solution.py:217
  31.1 0.4 y_step.7
  31.5 1.6 %collective-permute-start.22 = (f32[2,64,128]{2,1,0:T(8,128)S(1)}, f32[2,64,128]{2,1,0:T(8,128)S(1)}, u32[]{:S(2)}, u32[]{:S(2)}) collective-permute-start(f32[2,64,128]{2,1,0:T(8,128)S(1)} %get-tuple-element.98), channel_id=1, source_target_pairs={{0,1},{1,0},{2,3},{3,2},{4,5},{5,4},{6,7},{7,6},{8,9},{9,8},{10,11... | collective-permute-start | bytes 196616 | tf_op jit(solution)/shard_map/ppermute | solution.py:217
  33.1 0.7 y_step.5
  33.8 0.5 collective-permute-start.10
  34.3 0.3 collective-permute-start.23
  34.7 0.4 y_step.6
  35.1 2.5 %collective-permute-done.2.refs_2_ = f32[2,64,256]{2,1,0:T(8,128)S(1)} collective-permute-done((f32[2,64,256]{2,1,0:T(8,128)S(1)}, f32[2,64,256]{2,1,0:T(8,128)S(1)}, u32[]{:S(2)}, u32[]{:S(2)}) %collective-permute-start.2) | collective-permute-done | bytes 131104 | tf_op jit(solution)/shard_map/ppermute | solution.py:217
  37.6 1.6 %collective-permute-start.16 = (f32[2,64,256]{2,1,0:T(8,128)S(1)}, f32[2,64,256]{2,1,0:T(8,128)S(1)}, u32[]{:S(2)}, u32[]{:S(2)}) collective-permute-start(f32[2,64,256]{2,1,0:T(8,128)S(1)} %get-tuple-element.90), channel_id=1, source_target_pairs={{0,1},{1,0},{2,3},{3,2},{4,5},{5,4},{6,7},{7,6},{8,9},{9,8},{10,11... | collective-permute-start | bytes 393224 | tf_op jit(solution)/shard_map/ppermute | solution.py:217
  39.1 0.3 collective-permute-start.17
  39.5 1.6 %collective-permute-start.18 = (f32[2,64,256]{2,1,0:T(8,128)S(1)}, f32[2,64,256]{2,1,0:T(8,128)S(1)}, u32[]{:S(2)}, u32[]{:S(2)}) collective-permute-start(f32[2,64,256]{2,1,0:T(8,128)S(1)} %get-tuple-element.92), channel_id=1, source_target_pairs={{0,3},{1,2},{2,1},{3,0},{4,7},{5,6},{6,5},{7,4},{8,11},{9,10},{10,... | collective-permute-start | bytes 393224 | tf_op jit(solution)/shard_map/ppermute | solution.py:217
  41.1 2.1 %collective-permute-start.24 = (f32[2,64,128]{2,1,0:T(8,128)S(1)}, f32[2,64,128]{2,1,0:T(8,128)S(1)}, u32[]{:S(2)}, u32[]{:S(2)}) collective-permute-start(f32[2,64,128]{2,1,0:T(8,128)S(1)} %get-tuple-element.100), channel_id=1, source_target_pairs={{0,3},{1,2},{2,1},{3,0},{4,7},{5,6},{6,5},{7,4},{8,11},{9,10},{10,... | collective-permute-start | bytes 196616 | tf_op jit(solution)/shard_map/ppermute | solution.py:217
  43.2 0.1 dynamic_slice.3
  43.3 0.4 y_step.4
  43.7 11.4 %collective-permute-done.24.refs_3_ = f32[2,64,128]{2,1,0:T(8,128)S(1)} collective-permute-done((f32[2,64,128]{2,1,0:T(8,128)S(1)}, f32[2,64,128]{2,1,0:T(8,128)S(1)}, u32[]{:S(2)}, u32[]{:S(2)}) %collective-permute-start.24) | collective-permute-done | bytes 65568 | tf_op jit(solution)/shard_map/ppermute | solution.py:217
  55.1 2.6 %collective-permute-start.5 = (f32[2,64,256]{2,1,0:T(8,128)S(1)}, f32[2,64,256]{2,1,0:T(8,128)S(1)}, u32[]{:S(2)}, u32[]{:S(2)}) collective-permute-start(f32[2,64,256]{2,1,0:T(8,128)S(1)} %get-tuple-element.75), channel_id=1, source_target_pairs={{0,2},{1,3},{2,0},{3,1},{4,6},{5,7},{6,4},{7,5},{8,10},{9,11},{10,... | collective-permute-start | bytes 393224 | tf_op jit(solution)/shard_map/ppermute | solution.py:217
  57.6 0.9 %collective-permute-start.6 = (f32[2,64,256]{2,1,0:T(8,128)S(1)}, f32[2,64,256]{2,1,0:T(8,128)S(1)}, u32[]{:S(2)}, u32[]{:S(2)}) collective-permute-start(f32[2,64,256]{2,1,0:T(8,128)S(1)} %get-tuple-element.76), channel_id=1, source_target_pairs={{0,3},{1,2},{2,1},{3,0},{4,7},{5,6},{6,5},{7,4},{8,11},{9,10},{10,... | collective-permute-start | bytes 393224 | tf_op jit(solution)/shard_map/ppermute | solution.py:217
  58.6 1.4 %collective-permute-start.11 = (f32[2,64,384]{2,1,0:T(8,128)S(1)}, f32[2,64,384]{2,1,0:T(8,128)S(1)}, u32[]{:S(2)}, u32[]{:S(2)}) collective-permute-start(f32[2,64,384]{2,1,0:T(8,128)S(1)} %get-tuple-element.83), channel_id=1, source_target_pairs={{0,2},{1,3},{2,0},{3,1},{4,6},{5,7},{6,4},{7,5},{8,10},{9,11},{10,... | collective-permute-start | bytes 589832 | tf_op jit(solution)/shard_map/ppermute | solution.py:217
  60.0 0.9 %collective-permute-start.12 = (f32[2,64,384]{2,1,0:T(8,128)S(1)}, f32[2,64,384]{2,1,0:T(8,128)S(1)}, u32[]{:S(2)}, u32[]{:S(2)}) collective-permute-start(f32[2,64,384]{2,1,0:T(8,128)S(1)} %get-tuple-element.84), channel_id=1, source_target_pairs={{0,3},{1,2},{2,1},{3,0},{4,7},{5,6},{6,5},{7,4},{8,11},{9,10},{10,... | collective-permute-start | bytes 589832 | tf_op jit(solution)/shard_map/ppermute | solution.py:217
  60.9 0.1 add_add_fusion.refs_5_
  61.0 0.2 z_table.1.refs_4_
  61.2 1.7 %z_step.4.refs_8_ = f32[2,32,64,128]{3,2,1,0:T(8,128)} custom-call(f32[2,64,128]{2,1,0:T(8,128)S(1)} %get-tuple-element.97.refs_0_, f32[2,64,128]{2,1,0:T(8,128)S(1)} %collective-permute-done.22.refs_1_, f32[2,64,128]{2,1,0:T(8,128)S(1)} %collective-permute-done.23.refs_2_, f32[2,64,128]{2,1,0:T(8,128)S(1)} %collective-permute-done.24.refs_3_, ...), custom_call_target="tpu_custom_call" | custom-call | flops 201326592 | bytes 524288 | tf_op jit(solution)/shard_map/z_step/pallas_call | solution.py:326
  62.9 1.9 %z_step.5.refs_8_ = f32[2,32,64,128]{3,2,1,0:T(8,128)} custom-call(f32[2,64,256]{2,1,0:T(8,128)S(1)} %get-tuple-element.89.refs_0_, f32[2,64,256]{2,1,0:T(8,128)S(1)} %collective-permute-done.16.refs_1_, f32[2,64,256]{2,1,0:T(8,128)S(1)} %collective-permute-done.17.refs_2_, ...), custom_call_target="tpu_custom_call", output_to_operand_aliasing={{}: (8, {})} | custom-call | flops 402653184 | bytes 1048576 | tf_op jit(solution)/shard_map/z_step/pallas_call | solution.py:326
  64.8 16.4 %collective-permute-done.11.refs_2_ = f32[2,64,384]{2,1,0:T(8,128)S(1)} collective-permute-done((f32[2,64,384]{2,1,0:T(8,128)S(1)}, f32[2,64,384]{2,1,0:T(8,128)S(1)}, u32[]{:S(2)}, u32[]{:S(2)}) %collective-permute-start.11) | collective-permute-done | bytes 196640 | tf_op jit(solution)/shard_map/ppermute | solution.py:217
  81.3 4.5 %collective-permute-done.12.refs_3_ = f32[2,64,384]{2,1,0:T(8,128)S(1)} collective-permute-done((f32[2,64,384]{2,1,0:T(8,128)S(1)}, f32[2,64,384]{2,1,0:T(8,128)S(1)}, u32[]{:S(2)}, u32[]{:S(2)}) %collective-permute-start.12) | collective-permute-done | bytes 196640 | tf_op jit(solution)/shard_map/ppermute | solution.py:217
  85.8 2.2 %z_step.6.refs_8_ = f32[2,32,64,128]{3,2,1,0:T(8,128)} custom-call(f32[2,64,384]{2,1,0:T(8,128)S(1)} %get-tuple-element.81.refs_0_, f32[2,64,384]{2,1,0:T(8,128)S(1)} %collective-permute-done.10.refs_1_, f32[2,64,384]{2,1,0:T(8,128)S(1)} %collective-permute-done.11.refs_2_, ...), custom_call_target="tpu_custom_call", output_to_operand_aliasing={{}: (8, {})} | custom-call | flops 603979776 | bytes 1572864 | tf_op jit(solution)/shard_map/z_step/pallas_call | solution.py:326
  88.0 1.9 %z_step.7 = f32[2,32,64,128]{3,2,1,0:T(8,128)} custom-call(f32[2,64,256]{2,1,0:T(8,128)S(1)} %get-tuple-element.73.refs_0_, f32[2,64,256]{2,1,0:T(8,128)S(1)} %collective-permute-done.4.refs_1_, f32[2,64,256]{2,1,0:T(8,128)S(1)} %collective-permute-done.5.refs_2_, f32[2,64,256]{2,1,0:T(8,128)S(1)} %collective-permute-done.6.refs_3_, ...), custom_call_target="tpu_custom_call", output_to_operand_aliasing={{}: (8, {})} | custom-call | flops 402653184 | bytes 1048576 | tf_op jit(solution)/shard_map/z_step/pallas_call | solution.py:326
  (35 shorter events, 0.1 us)
Async XLA Ops:
  0.0 4.4 %collective-permute-start = (f32[2,1024,256]{2,1,0:T(8,128)}, f32[2,1024,256]{2,1,0:T(8,128)S(1)}, u32[]{:S(2)}, u32[]{:S(2)}) collective-permute-start(f32[2,1024,256]{2,1,0:T(8,128)} %bitcast.3), channel_id=1, source_target_pairs={{0,4},{4,0},{8,12},{12,8},{16,20},{20,16},{24,28},{28,24},{1,5},{5... | collective-permute-start | bytes 6291464 | tf_op jit(solution)/shard_map/ppermute | solution.py:280
  0.0 1.6 %copy-start.1 = (f32[2,256,32,32]{1,3,2,0:T(8,128)S(1)}, f32[2,256,32,32]{1,3,2,0:T(8,128)}, u32[]{:S(2)}) copy-start(f32[2,256,32,32]{1,3,2,0:T(8,128)} %param.9) | copy-start | bytes 6291460
  1.6 0.9 %copy-start.2 = (bf16[512,256]{1,0:T(8,128)(2,1)S(1)}, bf16[512,256]{1,0:T(8,128)(2,1)}, u32[]{:S(2)}) copy-start(bf16[512,256]{1,0:T(8,128)(2,1)} %constant.20.clone.table_ref) | copy-start | bytes 786436
  2.5 1.8 %copy-start.3 = (bf16[512,256]{1,0:T(8,128)(2,1)S(1)}, bf16[512,256]{1,0:T(8,128)(2,1)}, u32[]{:S(2)}) copy-start(bf16[512,256]{1,0:T(8,128)(2,1)} %constant.20.clone.table_ref) | copy-start | bytes 786436
  4.4 26.7 %copy-start = (bf16[256,768]{1,0:T(8,128)(2,1)S(1)}, bf16[256,768]{1,0:T(8,128)(2,1)}, u32[]{:S(2)}) copy-start(bf16[256,768]{1,0:T(8,128)(2,1)} %constant.21.clone.refs_4_) | copy-start | bytes 1179652
  5.5 37.7 %copy-start.9 = (f32[256]{0:T(256)S(1)}, f32[256]{0:T(256)}, u32[]{:S(2)}) copy-start(f32[256]{0:T(256)} %param.12) | copy-start | bytes 3076
  5.5 55.4 %copy-start.8 = (f32[128]{0:T(128)S(1)}, f32[128]{0:T(128)}, u32[]{:S(2)}) copy-start(f32[128]{0:T(128)} %param.13) | copy-start | bytes 1540
  5.5 55.5 %copy-start.4 = (bf16[128,128]{1,0:T(8,128)(2,1)S(1)}, bf16[128,128]{1,0:T(8,128)(2,1)}, u32[]{:S(2)}) copy-start(bf16[128,128]{1,0:T(8,128)(2,1)} %constant.22.clone.table_high) | copy-start | bytes 98308
  5.6 55.4 %copy-start.5 = (bf16[128,128]{1,0:T(8,128)(2,1)S(1)}, bf16[128,128]{1,0:T(8,128)(2,1)}, u32[]{:S(2)}) copy-start(bf16[128,128]{1,0:T(8,128)(2,1)} %constant.23.clone.table_low) | copy-start | bytes 98308
  5.6 6.6 %collective-permute-start.19 = (f32[2,64,128]{2,1,0:T(8,128)S(1)}, f32[2,64,128]{2,1,0:T(8,128)S(1)}, u32[]{:S(2)}, u32[]{:S(2)}) collective-permute-start(f32[2,64,128]{2,1,0:T(8,128)S(1)} %get-tuple-element.94), channel_id=1, source_target_pairs={{0,8},{4,12},{8,0},{12,4},{16,24},{20,28},{24,16},{28,20},{1,9},{5... | collective-permute-start | bytes 196616 | tf_op jit(solution)/shard_map/ppermute | solution.py:217
  7.1 5.5 %collective-permute-start.20 = (f32[2,64,128]{2,1,0:T(8,128)S(1)}, f32[2,64,128]{2,1,0:T(8,128)S(1)}, u32[]{:S(2)}, u32[]{:S(2)}) collective-permute-start(f32[2,64,128]{2,1,0:T(8,128)S(1)} %get-tuple-element.95), channel_id=1, source_target_pairs={{0,16},{4,20},{8,24},{12,28},{16,0},{20,4},{24,8},{28,12},{1,17},{... | collective-permute-start | bytes 196616 | tf_op jit(solution)/shard_map/ppermute | solution.py:217
  8.6 5.9 %collective-permute-start.21 = (f32[2,64,128]{2,1,0:T(8,128)S(1)}, f32[2,64,128]{2,1,0:T(8,128)S(1)}, u32[]{:S(2)}, u32[]{:S(2)}) collective-permute-start(f32[2,64,128]{2,1,0:T(8,128)S(1)} %get-tuple-element.96), channel_id=1, source_target_pairs={{0,24},{4,28},{8,16},{12,20},{16,8},{20,12},{24,0},{28,4},{1,25},{... | collective-permute-start | bytes 196616 | tf_op jit(solution)/shard_map/ppermute | solution.py:217
  9.1 19.3 %collective-permute-start.7 = (f32[2,64,384]{2,1,0:T(8,128)S(1)}, f32[2,64,384]{2,1,0:T(8,128)S(1)}, u32[]{:S(2)}, u32[]{:S(2)}) collective-permute-start(f32[2,64,384]{2,1,0:T(8,128)S(1)} %get-tuple-element.78), channel_id=1, source_target_pairs={{0,8},{4,12},{8,0},{12,4},{16,24},{20,28},{24,16},{28,20},{1,9},{5... | collective-permute-start | bytes 589832 | tf_op jit(solution)/shard_map/ppermute | solution.py:217
  10.6 18.3 %collective-permute-start.8 = (f32[2,64,384]{2,1,0:T(8,128)S(1)}, f32[2,64,384]{2,1,0:T(8,128)S(1)}, u32[]{:S(2)}, u32[]{:S(2)}) collective-permute-start(f32[2,64,384]{2,1,0:T(8,128)S(1)} %get-tuple-element.79), channel_id=1, source_target_pairs={{0,16},{4,20},{8,24},{12,28},{16,0},{20,4},{24,8},{28,12},{1,17},{... | collective-permute-start | bytes 589832 | tf_op jit(solution)/shard_map/ppermute | solution.py:217
  12.1 8.4 %collective-permute-start.1 = (f32[2,64,256]{2,1,0:T(8,128)S(1)}, f32[2,64,256]{2,1,0:T(8,128)S(1)}, u32[]{:S(2)}, u32[]{:S(2)}) collective-permute-start(f32[2,64,256]{2,1,0:T(8,128)S(1)} %get-tuple-element.70), channel_id=1, source_target_pairs={{0,8},{4,12},{8,0},{12,4},{16,24},{20,28},{24,16},{28,20},{1,9},{5... | collective-permute-start | bytes 393224 | tf_op jit(solution)/shard_map/ppermute | solution.py:217
  12.7 18.8 %collective-permute-start.9 = (f32[2,64,384]{2,1,0:T(8,128)S(1)}, f32[2,64,384]{2,1,0:T(8,128)S(1)}, u32[]{:S(2)}, u32[]{:S(2)}) collective-permute-start(f32[2,64,384]{2,1,0:T(8,128)S(1)} %get-tuple-element.80), channel_id=1, source_target_pairs={{0,24},{4,28},{8,16},{12,20},{16,8},{20,12},{24,0},{28,4},{1,25},{... | collective-permute-start | bytes 589832 | tf_op jit(solution)/shard_map/ppermute | solution.py:217
  14.5 12.1 %collective-permute-start.13 = (f32[2,64,256]{2,1,0:T(8,128)S(1)}, f32[2,64,256]{2,1,0:T(8,128)S(1)}, u32[]{:S(2)}, u32[]{:S(2)}) collective-permute-start(f32[2,64,256]{2,1,0:T(8,128)S(1)} %get-tuple-element.86), channel_id=1, source_target_pairs={{0,8},{4,12},{8,0},{12,4},{16,24},{20,28},{24,16},{28,20},{1,9},{5... | collective-permute-start | bytes 393224 | tf_op jit(solution)/shard_map/ppermute | solution.py:217
  20.6 13.2 %collective-permute-start.14 = (f32[2,64,256]{2,1,0:T(8,128)S(1)}, f32[2,64,256]{2,1,0:T(8,128)S(1)}, u32[]{:S(2)}, u32[]{:S(2)}) collective-permute-start(f32[2,64,256]{2,1,0:T(8,128)S(1)} %get-tuple-element.87), channel_id=1, source_target_pairs={{0,16},{4,20},{8,24},{12,28},{16,0},{20,4},{24,8},{28,12},{1,17},{... | collective-permute-start | bytes 393224 | tf_op jit(solution)/shard_map/ppermute | solution.py:217
  26.6 7.8 %collective-permute-start.15 = (f32[2,64,256]{2,1,0:T(8,128)S(1)}, f32[2,64,256]{2,1,0:T(8,128)S(1)}, u32[]{:S(2)}, u32[]{:S(2)}) collective-permute-start(f32[2,64,256]{2,1,0:T(8,128)S(1)} %get-tuple-element.88), channel_id=1, source_target_pairs={{0,24},{4,28},{8,16},{12,20},{16,8},{20,12},{24,0},{28,4},{1,25},{... | collective-permute-start | bytes 393224 | tf_op jit(solution)/shard_map/ppermute | solution.py:217
  28.4 9.1 %collective-permute-start.2 = (f32[2,64,256]{2,1,0:T(8,128)S(1)}, f32[2,64,256]{2,1,0:T(8,128)S(1)}, u32[]{:S(2)}, u32[]{:S(2)}) collective-permute-start(f32[2,64,256]{2,1,0:T(8,128)S(1)} %get-tuple-element.71), channel_id=1, source_target_pairs={{0,16},{4,20},{8,24},{12,28},{16,0},{20,4},{24,8},{28,12},{1,17},{... | collective-permute-start | bytes 393224 | tf_op jit(solution)/shard_map/ppermute | solution.py:217
  28.9 10.2 %collective-permute-start.3 = (f32[2,64,256]{2,1,0:T(8,128)S(1)}, f32[2,64,256]{2,1,0:T(8,128)S(1)}, u32[]{:S(2)}, u32[]{:S(2)}) collective-permute-start(f32[2,64,256]{2,1,0:T(8,128)S(1)} %get-tuple-element.72), channel_id=1, source_target_pairs={{0,24},{4,28},{8,16},{12,20},{16,8},{20,12},{24,0},{28,4},{1,25},{... | collective-permute-start | bytes 393224 | tf_op jit(solution)/shard_map/ppermute | solution.py:217
  31.5 8.0 %collective-permute-start.22 = (f32[2,64,128]{2,1,0:T(8,128)S(1)}, f32[2,64,128]{2,1,0:T(8,128)S(1)}, u32[]{:S(2)}, u32[]{:S(2)}) collective-permute-start(f32[2,64,128]{2,1,0:T(8,128)S(1)} %get-tuple-element.98), channel_id=1, source_target_pairs={{0,1},{1,0},{2,3},{3,2},{4,5},{5,4},{6,7},{7,6},{8,9},{9,8},{10,11... | collective-permute-start | bytes 196616 | tf_op jit(solution)/shard_map/ppermute | solution.py:217
  33.1 28.1 %copy-start.6 = (f32[256]{0:T(256)S(1)}, f32[256]{0:T(256)}, u32[]{:S(2)}) copy-start(f32[256]{0:T(256)} %refs_6_.7) | copy-start | bytes 3076
  33.1 28.1 %copy-start.7 = (f32[2,2]{1,0:T(2,128)S(1)}, f32[2,2]{1,0:T(2,128)}, u32[]{:S(2)}) copy-start(f32[2,2]{1,0:T(2,128)} %refs_7_.7) | copy-start | bytes 52
  33.8 26.2 %collective-permute-start.10 = (f32[2,64,384]{2,1,0:T(8,128)S(1)}, f32[2,64,384]{2,1,0:T(8,128)S(1)}, u32[]{:S(2)}, u32[]{:S(2)}) collective-permute-start(f32[2,64,384]{2,1,0:T(8,128)S(1)} %get-tuple-element.82), channel_id=1, source_target_pairs={{0,1},{1,0},{2,3},{3,2},{4,5},{5,4},{6,7},{7,6},{8,9},{9,8},{10,11... | collective-permute-start | bytes 589832 | tf_op jit(solution)/shard_map/ppermute | solution.py:217
  34.3 6.7 %collective-permute-start.23 = (f32[2,64,128]{2,1,0:T(8,128)S(1)}, f32[2,64,128]{2,1,0:T(8,128)S(1)}, u32[]{:S(2)}, u32[]{:S(2)}) collective-permute-start(f32[2,64,128]{2,1,0:T(8,128)S(1)} %get-tuple-element.99), channel_id=1, source_target_pairs={{0,2},{1,3},{2,0},{3,1},{4,6},{5,7},{6,4},{7,5},{8,10},{9,11},{10,... | collective-permute-start | bytes 196616 | tf_op jit(solution)/shard_map/ppermute | solution.py:217
  37.6 17.5 %collective-permute-start.16 = (f32[2,64,256]{2,1,0:T(8,128)S(1)}, f32[2,64,256]{2,1,0:T(8,128)S(1)}, u32[]{:S(2)}, u32[]{:S(2)}) collective-permute-start(f32[2,64,256]{2,1,0:T(8,128)S(1)} %get-tuple-element.90), channel_id=1, source_target_pairs={{0,1},{1,0},{2,3},{3,2},{4,5},{5,4},{6,7},{7,6},{8,9},{9,8},{10,11... | collective-permute-start | bytes 393224 | tf_op jit(solution)/shard_map/ppermute | solution.py:217
  39.1 18.5 %collective-permute-start.17 = (f32[2,64,256]{2,1,0:T(8,128)S(1)}, f32[2,64,256]{2,1,0:T(8,128)S(1)}, u32[]{:S(2)}, u32[]{:S(2)}) collective-permute-start(f32[2,64,256]{2,1,0:T(8,128)S(1)} %get-tuple-element.91), channel_id=1, source_target_pairs={{0,2},{1,3},{2,0},{3,1},{4,6},{5,7},{6,4},{7,5},{8,10},{9,11},{10,... | collective-permute-start | bytes 393224 | tf_op jit(solution)/shard_map/ppermute | solution.py:217
  39.5 19.1 %collective-permute-start.18 = (f32[2,64,256]{2,1,0:T(8,128)S(1)}, f32[2,64,256]{2,1,0:T(8,128)S(1)}, u32[]{:S(2)}, u32[]{:S(2)}) collective-permute-start(f32[2,64,256]{2,1,0:T(8,128)S(1)} %get-tuple-element.92), channel_id=1, source_target_pairs={{0,3},{1,2},{2,1},{3,0},{4,7},{5,6},{6,5},{7,4},{8,11},{9,10},{10,... | collective-permute-start | bytes 393224 | tf_op jit(solution)/shard_map/ppermute | solution.py:217
  41.1 14.0 %collective-permute-start.24 = (f32[2,64,128]{2,1,0:T(8,128)S(1)}, f32[2,64,128]{2,1,0:T(8,128)S(1)}, u32[]{:S(2)}, u32[]{:S(2)}) collective-permute-start(f32[2,64,128]{2,1,0:T(8,128)S(1)} %get-tuple-element.100), channel_id=1, source_target_pairs={{0,3},{1,2},{2,1},{3,0},{4,7},{5,6},{6,5},{7,4},{8,11},{9,10},{10,... | collective-permute-start | bytes 196616 | tf_op jit(solution)/shard_map/ppermute | solution.py:217
  55.1 33.0 %collective-permute-start.4 = (f32[2,64,256]{2,1,0:T(8,128)S(1)}, f32[2,64,256]{2,1,0:T(8,128)S(1)}, u32[]{:S(2)}, u32[]{:S(2)}) collective-permute-start(f32[2,64,256]{2,1,0:T(8,128)S(1)} %get-tuple-element.74), channel_id=1, source_target_pairs={{0,1},{1,0},{2,3},{3,2},{4,5},{5,4},{6,7},{7,6},{8,9},{9,8},{10,11... | collective-permute-start | bytes 393224 | tf_op jit(solution)/shard_map/ppermute | solution.py:217
  55.1 33.0 %collective-permute-start.5 = (f32[2,64,256]{2,1,0:T(8,128)S(1)}, f32[2,64,256]{2,1,0:T(8,128)S(1)}, u32[]{:S(2)}, u32[]{:S(2)}) collective-permute-start(f32[2,64,256]{2,1,0:T(8,128)S(1)} %get-tuple-element.75), channel_id=1, source_target_pairs={{0,2},{1,3},{2,0},{3,1},{4,6},{5,7},{6,4},{7,5},{8,10},{9,11},{10,... | collective-permute-start | bytes 393224 | tf_op jit(solution)/shard_map/ppermute | solution.py:217
  57.6 30.4 %collective-permute-start.6 = (f32[2,64,256]{2,1,0:T(8,128)S(1)}, f32[2,64,256]{2,1,0:T(8,128)S(1)}, u32[]{:S(2)}, u32[]{:S(2)}) collective-permute-start(f32[2,64,256]{2,1,0:T(8,128)S(1)} %get-tuple-element.76), channel_id=1, source_target_pairs={{0,3},{1,2},{2,1},{3,0},{4,7},{5,6},{6,5},{7,4},{8,11},{9,10},{10,... | collective-permute-start | bytes 393224 | tf_op jit(solution)/shard_map/ppermute | solution.py:217
  58.6 22.7 %collective-permute-start.11 = (f32[2,64,384]{2,1,0:T(8,128)S(1)}, f32[2,64,384]{2,1,0:T(8,128)S(1)}, u32[]{:S(2)}, u32[]{:S(2)}) collective-permute-start(f32[2,64,384]{2,1,0:T(8,128)S(1)} %get-tuple-element.83), channel_id=1, source_target_pairs={{0,2},{1,3},{2,0},{3,1},{4,6},{5,7},{6,4},{7,5},{8,10},{9,11},{10,... | collective-permute-start | bytes 589832 | tf_op jit(solution)/shard_map/ppermute | solution.py:217
  60.0 25.8 %collective-permute-start.12 = (f32[2,64,384]{2,1,0:T(8,128)S(1)}, f32[2,64,384]{2,1,0:T(8,128)S(1)}, u32[]{:S(2)}, u32[]{:S(2)}) collective-permute-start(f32[2,64,384]{2,1,0:T(8,128)S(1)} %get-tuple-element.84), channel_id=1, source_target_pairs={{0,3},{1,2},{2,1},{3,0},{4,7},{5,6},{6,5},{7,4},{8,11},{9,10},{10,... | collective-permute-start | bytes 589832 | tf_op jit(solution)/shard_map/ppermute | solution.py:217
where the time goes:
time: 91.1 us; the launch traced here: 90 us
  waiting for transfers between devices  45.2 us (50%)
  starting transfers between devices  29.1 us (32%)
  Pallas kernels  12.8 us (14%)
  local copies, waits for them, and re-layouts  2.66 us (3%)
    ppermute x24, waiting for transfers between devices, exchange(): moved.append(lax.ppermute(arrays[k], axis, pairs))  45.2 us
    ppermute x24, starting transfers between devices, exchange(): moved.append(lax.ppermute(arrays[k], axis, pairs))  29.1 us
    pallas_call x4, Pallas kernels, z_step(): pl.pallas_call(functools.partial(z_kernel, cols, groups, firsts[q], has_p...  7.78 us
    pallas_call x2, Pallas kernels, x_step(): pl.pallas_call(functools.partial(x_kernel, chips, units, groups, own), ou...  2.89 us
    unnamed x20, local copies, waits for them, and re-layouts  2.58 us
    pallas_call x4, Pallas kernels, y_step(): pl.pallas_call(functools.partial(y_kernel, chips, cols), out_shape=[shape...  1.92 us
  transfers between devices with their start and end apart: 25, of which 8 were waited for; matrix products, arithmetic and copies ran while one was open for 0% of the time, Pallas kernels for 11%

commit v1 on v0

--- a/solution.py
+++ b/solution.py
@@ -11,13 +11,11 @@
 
 LANES = 128
 SPARE = 4 << 20
-SHARES = (1, 2, 3, 2)
+SHARES = (1, 2, 2, 3)
 
 
 ANY = pl.BlockSpec(memory_space=pl.ANY)
 VMEM = pl.BlockSpec(memory_space=pltpu.VMEM)
-HBM = pl.BlockSpec(memory_space=pltpu.HBM)
-SMEM = pl.BlockSpec(memory_space=pltpu.SMEM)
 
 
 def mode_table(count):
@@ -75,23 +73,12 @@
     me = lax.axis_index("row")
     pair = me % 2
     owner = pair if first else 1 - pair
-    if first:
-        source, sems = refs[1:]
-        loads = [
-            pltpu.make_async_copy(lines.at[f], source.at[f], sems.at[f]) for f in range(fields)
-        ]
-        for load in loads:
-            load.start()
-    else:
-        source = lines
     depth = table_ref.shape[0] // 2
     table = table_ref[pl.ds(pl.multiple_of(pair * depth, depth), depth), :]
     half = depth // 2
     tall = scratch.shape[2] // blocks
     for f in range(fields):
-        if first:
-            loads[f].wait()
-        high, low = split(source[f])
+        high, low = split(lines[f])
         both = dot(table, high, (1, 1))
         result = both[:half] + both[half:] + dot(table[:half], low, (1, 1))
         for j in range(half // tall):
@@ -158,12 +145,11 @@
 
 def z_kernel(peers, groups, first, has_prior, *refs):
     ins, refs = refs[:peers], refs[peers:]
-    wide, syz, symbol_x, coupling = refs[:4]
+    wide, syz, sx, coupling = refs[:4]
     modes, mixed, sems = refs[4 + has_prior :]
     fields, share, lanes = ins[0].shape
     units = lanes // LANES
     out_width = wide.shape[1] // groups
-    row = lax.axis_index("row")
     parts = []
     for hi in range(units):
         for f in range(fields):
@@ -177,8 +163,7 @@
     for hi in range(units):
         for g in range(groups):
             kx = hi * groups + g
-            line = row * (symbol_x.shape[0] // lax.axis_size("row")) + first + kx
-            weight = 1.0 / (syz[...] + symbol_x[line])
+            weight = 1.0 / (syz[...] + sx[first + kx : first + kx + 1, :])
             rest = 1.0 - weight
             mine = [
                 old[
@@ -188,9 +173,10 @@
                 for f in range(fields)
             ]
             for a in range(fields):
-                mix = coupling[a, 0] * mine[0]
+                pair = [coupling[a * fields + b : a * fields + b + 1, :] for b in range(fields)]
+                mix = pair[0] * mine[0]
                 for b in range(1, fields):
-                    mix = mix + coupling[a, b] * mine[b]
+                    mix = mix + pair[b] * mine[b]
                 mixed[a, kx] = weight * mine[a] + rest * mix
         stores.append(
             pltpu.make_async_copy(
@@ -259,19 +245,14 @@
             return pl.pallas_call(
                 functools.partial(x_kernel, chips, units, groups, own),
                 out_shape=message_shapes,
-                in_specs=[HBM if own else VMEM, VMEM] + [VMEM] * len(sent),
+                in_specs=[VMEM] * (2 + len(sent)),
                 out_specs=[VMEM] * len(message_shapes),
                 input_output_aliases={2 + i: i for i in range(len(sent))},
                 scratch_shapes=[
                     pltpu.VMEM(
                         (fields, share_kx * chips // tall, blocks * tall, LANES), f32
                     )
-                ]
-                + [
-                    pltpu.VMEM(lines.shape, f32),
-                    pltpu.SemaphoreType.DMA((fields,)),
-                ]
-                * own,
+                ],
                 cost_estimate=cost(3 * lines.size * size_x, 8 * lines.size),
                 compiler_params=limit((lines.shape, 24)),
                 name="x_step",
@@ -318,6 +299,9 @@
         )(*table_z)
         part_y = lax.dynamic_slice_in_dim(symbol_y, lax.axis_index("col") * share_ky, share_ky)
         syz = 1.0 + (part_y[:, None] + symbol_z[None, :])
+        part_x = lax.dynamic_slice_in_dim(symbol_x, lax.axis_index("row") * share_kx, share_kx)
+        sx = jnp.broadcast_to(part_x[:, None], (share_kx, size_z))
+        mix = jnp.broadcast_to(coupling.reshape(-1, 1), (fields * fields, size_z))
         out_shape = jax.ShapeDtypeStruct((fields, share_kx, share_ky, size_z), f32)
 
         def z_step(q, arrays, prior):
@@ -326,7 +310,7 @@
             return pl.pallas_call(
                 functools.partial(z_kernel, cols, groups, firsts[q], has_prior),
                 out_shape=out_shape,
-                in_specs=[VMEM] * (cols + 2) + [SMEM] * 2 + [ANY] * has_prior,
+                in_specs=[VMEM] * (cols + 4) + [ANY] * has_prior,
                 out_specs=ANY,
                 input_output_aliases={cols + 4: 0} if has_prior else {},
                 scratch_shapes=[
@@ -341,7 +325,7 @@
                     ((cols, fields, share_ky, lanes), 24), (wide_shape, 4)
                 ),
                 name="z_step",
-            )(*arrays, wide, syz, symbol_x, coupling, *([prior] if has_prior else []))
+            )(*arrays, wide, syz, sx, mix, *([prior] if has_prior else []))
 
         lines_z = []
         for q in range(n_chunk):

time: 91.1 us -> 83 us (0.911)
  waiting for transfers between devices: 45.2 us -> 36.1 us
  starting transfers between devices: 29.1 us -> 30.9 us
  Pallas kernels: 12.8 us -> 11.3 us
    ppermute x24, waiting for transfers between devices: 45.2 us -> 35.4 us  [exchange(): moved.append(lax.ppermute(arrays[k], axis, pairs))]
    pallas_call x4, Pallas kernels: 7.78 us -> 5.61 us  [z_step(): pl.pallas_call(functools.partial(z_kernel, cols, groups, firsts[q], has_p...]
    ppermute x24, starting transfers between devices: 29.1 us -> 30.9 us  [exchange(): moved.append(lax.ppermute(arrays[k], axis, pairs))]
    pallas_call x4, Pallas kernels: 1.92 us -> 3.24 us  [y_step(): pl.pallas_call(functools.partial(y_kernel, chips, cols), out_shape=[shape...]
  transfers between devices with their start and end apart: 25 -> 25, of which waited for: 8 -> 8; matrix products, arithmetic and copies ran while one was open for 0% -> 1% of each run, Pallas kernels for 11% -> 10%
where the time goes in v1:
time: 83 us; the launch traced here: 81.5 us
  waiting for transfers between devices  36.1 us (43%)
  starting transfers between devices  30.9 us (37%)
  Pallas kernels  11.3 us (14%)
  local copies, waits for them, and re-layouts  2.96 us (4%)
    ppermute x24, waiting for transfers between devices, exchange(): moved.append(lax.ppermute(arrays[k], axis, pairs))  35.4 us
    ppermute x24, starting transfers between devices, exchange(): moved.append(lax.ppermute(arrays[k], axis, pairs))  30.9 us
    pallas_call x4, Pallas kernels, z_step(): pl.pallas_call(functools.partial(z_kernel, cols, groups, firsts[q], has_p...  5.61 us
    pallas_call x4, Pallas kernels, y_step(): pl.pallas_call(functools.partial(y_kernel, chips, cols), out_shape=[shape...  3.24 us
    unnamed x20, local copies, waits for them, and re-layouts  2.59 us
    pallas_call x2, Pallas kernels, x_step(): pl.pallas_call(functools.partial(x_kernel, chips, units, groups, own), ou...  2.28 us
  transfers between devices with their start and end apart: 25, of which 8 were waited for; matrix products, arithmetic and copies ran while one was open for 1% of the time, Pallas kernels for 10%

profile of v1, /device:TPU:16, one launch (start us, length us, event | category | flops | bytes accessed | tf_op | source)
XLA Modules:
  0.0 81.5 jit_solution(4122708655742040747)
XLA Ops:
  0.0 1.6 %copy-done.1 = f32[2,256,32,32]{1,3,2,0:T(8,128)S(1)} copy-done((f32[2,256,32,32]{1,3,2,0:T(8,128)S(1)}, f32[2,256,32,32]{1,3,2,0:T(8,128)}, u32[]{:S(2)}) %copy-start.1) | copy-done | bytes 2097176
  1.6 0.9 %copy-done.2 = bf16[512,256]{1,0:T(8,128)(2,1)S(1)} copy-done((bf16[512,256]{1,0:T(8,128)(2,1)S(1)}, bf16[512,256]{1,0:T(8,128)(2,1)}, u32[]{:S(2)}) %copy-start.2) | copy-done | bytes 262168
  2.5 1.1 %x_step.2 = (f32[2,64,128]{2,1,0:T(8,128)S(1)}, f32[2,64,128]{2,1,0:T(8,128)S(1)}, f32[2,64,128]{2,1,0:T(8,128)S(1)}, f32[2,64,128]{2,1,0:T(8,128)S(1)}, f32[2,6...) custom-call(f32[2,1024,256]{2,1,0:T(8,128)S(1)} %bitcast.4, ...), custom_call_target="tpu_custom_call" | custom-call | flops 402653184 | bytes 4194304 | tf_op jit(solution)/shard_map/x_step/pallas_call | solution.py:245
  3.7 0.7 collective-permute-done.lines
  4.4 1.1 %x_step.3 = (f32[2,64,128]{2,1,0:T(8,128)S(1)}, f32[2,64,128]{2,1,0:T(8,128)S(1)}, f32[2,64,128]{2,1,0:T(8,128)S(1)}, f32[2,64,128]{2,1,0:T(8,128)S(1)}, f32[2,6...) custom-call(f32[2,1024,256]{2,1,0:T(8,128)S(1)} %collective-permute-, ...), custom_call_target="tpu_custom_call", output_to_operand_aliasing={{0}: (2, {}), {1}: (3, {}), {2}: (4, {}), {3}: (5, {}), {4}... | custom-call | flops 402653184 | bytes 4194304 | tf_op jit(solution)/shard_map/x_step/pallas_call | solution.py:245
  5.6 1.6 %collective-permute-start.19 = (f32[2,64,128]{2,1,0:T(8,128)S(1)}, f32[2,64,128]{2,1,0:T(8,128)S(1)}, u32[]{:S(2)}, u32[]{:S(2)}) collective-permute-start(f32[2,64,128]{2,1,0:T(8,128)S(1)} %get-tuple-element.94), channel_id=1, source_target_pairs={{0,8},{4,12},{8,0},{12,4},{16,24},{20,28},{24,16},{28,20},{1,9},{5... | collective-permute-start | bytes 196616 | tf_op jit(solution)/shard_map/ppermute | solution.py:203
  7.2 1.5 %collective-permute-start.20 = (f32[2,64,128]{2,1,0:T(8,128)S(1)}, f32[2,64,128]{2,1,0:T(8,128)S(1)}, u32[]{:S(2)}, u32[]{:S(2)}) collective-permute-start(f32[2,64,128]{2,1,0:T(8,128)S(1)} %get-tuple-element.95), channel_id=1, source_target_pairs={{0,16},{4,20},{8,24},{12,28},{16,0},{20,4},{24,8},{28,12},{1,17},{... | collective-permute-start | bytes 196616 | tf_op jit(solution)/shard_map/ppermute | solution.py:203
  8.7 0.5 collective-permute-start.7
  9.2 0.5 collective-permute-start.8
  9.7 2.4 %collective-permute-start.9 = (f32[2,64,256]{2,1,0:T(8,128)S(1)}, f32[2,64,256]{2,1,0:T(8,128)S(1)}, u32[]{:S(2)}, u32[]{:S(2)}) collective-permute-start(f32[2,64,256]{2,1,0:T(8,128)S(1)} %get-tuple-element.80), channel_id=1, source_target_pairs={{0,24},{4,28},{8,16},{12,20},{16,8},{20,12},{24,0},{28,4},{1,25},{... | collective-permute-start | bytes 393224 | tf_op jit(solution)/shard_map/ppermute | solution.py:203
  12.2 0.5 collective-permute-start.13
  12.7 1.4 %collective-permute-start.21 = (f32[2,64,128]{2,1,0:T(8,128)S(1)}, f32[2,64,128]{2,1,0:T(8,128)S(1)}, u32[]{:S(2)}, u32[]{:S(2)}) collective-permute-start(f32[2,64,128]{2,1,0:T(8,128)S(1)} %get-tuple-element.96), channel_id=1, source_target_pairs={{0,24},{4,28},{8,16},{12,20},{16,8},{20,12},{24,0},{28,4},{1,25},{... | collective-permute-start | bytes 196616 | tf_op jit(solution)/shard_map/ppermute | solution.py:203
  14.1 6.6 %collective-permute-done.21.refs_3_ = f32[2,64,128]{2,1,0:T(8,128)S(1)} collective-permute-done((f32[2,64,128]{2,1,0:T(8,128)S(1)}, f32[2,64,128]{2,1,0:T(8,128)S(1)}, u32[]{:S(2)}, u32[]{:S(2)}) %collective-permute-start.21) | collective-permute-done | bytes 65568 | tf_op jit(solution)/shard_map/ppermute | solution.py:203
  20.7 1.4 %collective-permute-start.14 = (f32[2,64,256]{2,1,0:T(8,128)S(1)}, f32[2,64,256]{2,1,0:T(8,128)S(1)}, u32[]{:S(2)}, u32[]{:S(2)}) collective-permute-start(f32[2,64,256]{2,1,0:T(8,128)S(1)} %get-tuple-element.87), channel_id=1, source_target_pairs={{0,16},{4,20},{8,24},{12,28},{16,0},{20,4},{24,8},{28,12},{1,17},{... | collective-permute-start | bytes 393224 | tf_op jit(solution)/shard_map/ppermute | solution.py:203
  22.1 1.4 %collective-permute-start.15 = (f32[2,64,256]{2,1,0:T(8,128)S(1)}, f32[2,64,256]{2,1,0:T(8,128)S(1)}, u32[]{:S(2)}, u32[]{:S(2)}) collective-permute-start(f32[2,64,256]{2,1,0:T(8,128)S(1)} %get-tuple-element.88), channel_id=1, source_target_pairs={{0,24},{4,28},{8,16},{12,20},{16,8},{20,12},{24,0},{28,4},{1,25},{... | collective-permute-start | bytes 393224 | tf_op jit(solution)/shard_map/ppermute | solution.py:203
  23.6 0.6 collective-permute-start.1
  24.2 1.4 %collective-permute-start.2 = (f32[2,64,384]{2,1,0:T(8,128)S(1)}, f32[2,64,384]{2,1,0:T(8,128)S(1)}, u32[]{:S(2)}, u32[]{:S(2)}) collective-permute-start(f32[2,64,384]{2,1,0:T(8,128)S(1)} %get-tuple-element.71), channel_id=1, source_target_pairs={{0,16},{4,20},{8,24},{12,28},{16,0},{20,4},{24,8},{28,12},{1,17},{... | collective-permute-start | bytes 589832 | tf_op jit(solution)/shard_map/ppermute | solution.py:203
  25.6 1.4 %collective-permute-start.3 = (f32[2,64,384]{2,1,0:T(8,128)S(1)}, f32[2,64,384]{2,1,0:T(8,128)S(1)}, u32[]{:S(2)}, u32[]{:S(2)}) collective-permute-start(f32[2,64,384]{2,1,0:T(8,128)S(1)} %get-tuple-element.72), channel_id=1, source_target_pairs={{0,24},{4,28},{8,16},{12,20},{16,8},{20,12},{24,0},{28,4},{1,25},{... | collective-permute-start | bytes 589832 | tf_op jit(solution)/shard_map/ppermute | solution.py:203
  27.1 0.4 y_step.7
  27.5 3.2 %collective-permute-done.14.refs_2_ = f32[2,64,256]{2,1,0:T(8,128)S(1)} collective-permute-done((f32[2,64,256]{2,1,0:T(8,128)S(1)}, f32[2,64,256]{2,1,0:T(8,128)S(1)}, u32[]{:S(2)}, u32[]{:S(2)}) %collective-permute-start.14) | collective-permute-done | bytes 131104 | tf_op jit(solution)/shard_map/ppermute | solution.py:203
  30.7 1.6 %collective-permute-start.22 = (f32[2,64,128]{2,1,0:T(8,128)S(1)}, f32[2,64,128]{2,1,0:T(8,128)S(1)}, u32[]{:S(2)}, u32[]{:S(2)}) collective-permute-start(f32[2,64,128]{2,1,0:T(8,128)S(1)} %get-tuple-element.98), channel_id=1, source_target_pairs={{0,1},{1,0},{2,3},{3,2},{4,5},{5,4},{6,7},{7,6},{8,9},{9,8},{10,11... | collective-permute-start | bytes 196616 | tf_op jit(solution)/shard_map/ppermute | solution.py:203
  32.3 0.3 collective-permute-start.23
  32.6 1.1 %y_step.5 = (f32[2,64,256]{2,1,0:T(8,128)S(1)}, f32[2,64,256]{2,1,0:T(8,128)}, f32[2,64,256]{2,1,0:T(8,128)S(1)}, f32[2,64,256]{2,1,0:T(8,128)S(1)}) custom-call(f32[2,64,256]{2,1,0:T(8,128)S(1)} %get-tuple-element.77.refs_0_, f32[2,64,256]{2,1,0:T(8,128)S(1)} %collective-permute-done.7.refs_1_, f32[2,64,256]{2,1,0:T(8,128)S(1)} %collective-permute-done.8.refs_2_, ...), custom_call_target="tpu_custom_call" | custom-call | flops 201326592 | bytes 1048576 | tf_op jit(solution)/shard_map/y_step/pallas_call | solution.py:276
  33.7 1.1 %y_step.6 = (f32[2,64,256]{2,1,0:T(8,128)S(1)}, f32[2,64,256]{2,1,0:T(8,128)}, f32[2,64,256]{2,1,0:T(8,128)}, f32[2,64,256]{2,1,0:T(8,128)S(1)}) custom-call(f32[2,64,256]{2,1,0:T(8,128)S(1)} %get-tuple-element.85.refs_0_, f32[2,64,256]{2,1,0:T(8,128)S(1)} %collective-permute-done.13.refs_1_, f32[2,64,256]{2,1,0:T(8,128)S(1)} %collective-permute-done.14.refs_2_, ...), custom_call_target="tpu_custom_call" | custom-call | flops 201326592 | bytes 1048576 | tf_op jit(solution)/shard_map/y_step/pallas_call | solution.py:276
  34.8 0.9 %collective-permute-done.22.refs_1_ = f32[2,64,128]{2,1,0:T(8,128)S(1)} collective-permute-done((f32[2,64,128]{2,1,0:T(8,128)S(1)}, f32[2,64,128]{2,1,0:T(8,128)S(1)}, u32[]{:S(2)}, u32[]{:S(2)}) %collective-permute-start.22) | collective-permute-done | bytes 65568 | tf_op jit(solution)/shard_map/ppermute | solution.py:203
  35.7 2.4 %collective-permute-start.10 = (f32[2,64,256]{2,1,0:T(8,128)}, f32[2,64,256]{2,1,0:T(8,128)S(1)}, u32[]{:S(2)}, u32[]{:S(2)}) collective-permute-start(f32[2,64,256]{2,1,0:T(8,128)} %get-tuple-element.82), channel_id=1, source_target_pairs={{0,1},{1,0},{2,3},{3,2},{4,5},{5,4},{6,7},{7,6},{8,9},{9,8},{10,11... | collective-permute-start | bytes 393224 | tf_op jit(solution)/shard_map/ppermute | solution.py:203
  38.1 1.1 %collective-permute-done.23.refs_2_ = f32[2,64,128]{2,1,0:T(8,128)S(1)} collective-permute-done((f32[2,64,128]{2,1,0:T(8,128)S(1)}, f32[2,64,128]{2,1,0:T(8,128)S(1)}, u32[]{:S(2)}, u32[]{:S(2)}) %collective-permute-start.23) | collective-permute-done | bytes 65568 | tf_op jit(solution)/shard_map/ppermute | solution.py:203
  39.2 3.6 %collective-permute-start.16 = (f32[2,64,256]{2,1,0:T(8,128)}, f32[2,64,256]{2,1,0:T(8,128)S(1)}, u32[]{:S(2)}, u32[]{:S(2)}) collective-permute-start(f32[2,64,256]{2,1,0:T(8,128)} %get-tuple-element.90), channel_id=1, source_target_pairs={{0,1},{1,0},{2,3},{3,2},{4,5},{5,4},{6,7},{7,6},{8,9},{9,8},{10,11... | collective-permute-start | bytes 393224 | tf_op jit(solution)/shard_map/ppermute | solution.py:203
  42.8 1.4 %collective-permute-start.18 = (f32[2,64,256]{2,1,0:T(8,128)S(1)}, f32[2,64,256]{2,1,0:T(8,128)S(1)}, u32[]{:S(2)}, u32[]{:S(2)}) collective-permute-start(f32[2,64,256]{2,1,0:T(8,128)S(1)} %get-tuple-element.92), channel_id=1, source_target_pairs={{0,3},{1,2},{2,1},{3,0},{4,7},{5,6},{6,5},{7,4},{8,11},{9,10},{10,... | collective-permute-start | bytes 393224 | tf_op jit(solution)/shard_map/ppermute | solution.py:203
  44.3 0.6 collective-permute-start.24
  44.9 0.1 dynamic_slice.6
  45.0 0.7 y_step.4
  45.7 17.9 %collective-permute-done.24.refs_3_ = f32[2,64,128]{2,1,0:T(8,128)S(1)} collective-permute-done((f32[2,64,128]{2,1,0:T(8,128)S(1)}, f32[2,64,128]{2,1,0:T(8,128)S(1)}, u32[]{:S(2)}, u32[]{:S(2)}) %collective-permute-start.24) | collective-permute-done | bytes 65568 | tf_op jit(solution)/shard_map/ppermute | solution.py:203
  63.6 0.6 collective-permute-start.12
  64.2 3.7 %collective-permute-start.4 = (f32[2,64,384]{2,1,0:T(8,128)S(1)}, f32[2,64,384]{2,1,0:T(8,128)S(1)}, u32[]{:S(2)}, u32[]{:S(2)}) collective-permute-start(f32[2,64,384]{2,1,0:T(8,128)S(1)} %get-tuple-element.74), channel_id=1, source_target_pairs={{0,1},{1,0},{2,3},{3,2},{4,5},{5,4},{6,7},{7,6},{8,9},{9,8},{10,11... | collective-permute-start | bytes 589832 | tf_op jit(solution)/shard_map/ppermute | solution.py:203
  68.0 0.1 collective-permute-start.5
  68.1 1.4 %collective-permute-start.6 = (f32[2,64,384]{2,1,0:T(8,128)S(1)}, f32[2,64,384]{2,1,0:T(8,128)S(1)}, u32[]{:S(2)}, u32[]{:S(2)}) collective-permute-start(f32[2,64,384]{2,1,0:T(8,128)S(1)} %get-tuple-element.76), channel_id=1, source_target_pairs={{0,3},{1,2},{2,1},{3,0},{4,7},{5,6},{6,5},{7,4},{8,11},{9,10},{10,... | collective-permute-start | bytes 589832 | tf_op jit(solution)/shard_map/ppermute | solution.py:203
  69.5 0.1 add_add_fusion.refs_5_
  69.6 0.1 broadcast_in_dim.7
  69.7 0.1 dynamic_slice.7
  69.8 0.2 z_table.1.refs_4_
  69.9 0.1 broadcast_in_dim.6.refs_6_
  70.1 1.1 %z_step.4.refs_8_ = f32[2,32,64,128]{3,2,1,0:T(8,128)} custom-call(f32[2,64,128]{2,1,0:T(8,128)S(1)} %get-tuple-element.97.refs_0_, f32[2,64,128]{2,1,0:T(8,128)S(1)} %collective-permute-done.22.refs_1_, f32[2,64,128]{2,1,0:T(8,128)S(1)} %collective-permute-done.23.refs_2_, f32[2,64,128]{2,1,0:T(8,128)S(1)} %collective-permute-done.24.refs_3_, ...), custom_call_target="tpu_custom_call" | custom-call | flops 201326592 | bytes 524288 | tf_op jit(solution)/shard_map/z_step/pallas_call | solution.py:310
  71.2 1.4 %z_step.5.refs_8_ = f32[2,32,64,128]{3,2,1,0:T(8,128)} custom-call(f32[2,64,256]{2,1,0:T(8,128)S(1)} %get-tuple-element.89.refs_0_, f32[2,64,256]{2,1,0:T(8,128)S(1)} %collective-permute-done.16.refs_1_, f32[2,64,256]{2,1,0:T(8,128)S(1)} %collective-permute-done.17.refs_2_, ...), custom_call_target="tpu_custom_call", output_to_operand_aliasing={{}: (8, {})} | custom-call | flops 402653184 | bytes 1048576 | tf_op jit(solution)/shard_map/z_step/pallas_call | solution.py:310
  72.6 1.4 %z_step.6.refs_8_ = f32[2,32,64,128]{3,2,1,0:T(8,128)} custom-call(f32[2,64,256]{2,1,0:T(8,128)S(1)} %get-tuple-element.81.refs_0_, f32[2,64,256]{2,1,0:T(8,128)S(1)} %collective-permute-done.10.refs_1_, f32[2,64,256]{2,1,0:T(8,128)S(1)} %collective-permute-done.11.refs_2_, ...), custom_call_target="tpu_custom_call", output_to_operand_aliasing={{}: (8, {})} | custom-call | flops 402653184 | bytes 1048576 | tf_op jit(solution)/shard_map/z_step/pallas_call | solution.py:310
  74.1 2.6 %collective-permute-done.5.refs_2_ = f32[2,64,384]{2,1,0:T(8,128)S(1)} collective-permute-done((f32[2,64,384]{2,1,0:T(8,128)S(1)}, f32[2,64,384]{2,1,0:T(8,128)S(1)}, u32[]{:S(2)}, u32[]{:S(2)}) %collective-permute-start.5) | collective-permute-done | bytes 196640 | tf_op jit(solution)/shard_map/ppermute | solution.py:203
  76.6 3.2 %collective-permute-done.6.refs_3_ = f32[2,64,384]{2,1,0:T(8,128)S(1)} collective-permute-done((f32[2,64,384]{2,1,0:T(8,128)S(1)}, f32[2,64,384]{2,1,0:T(8,128)S(1)}, u32[]{:S(2)}, u32[]{:S(2)}) %collective-permute-start.6) | collective-permute-done | bytes 196640 | tf_op jit(solution)/shard_map/ppermute | solution.py:203
  79.8 1.7 %z_step.7 = f32[2,32,64,128]{3,2,1,0:T(8,128)} custom-call(f32[2,64,384]{2,1,0:T(8,128)S(1)} %get-tuple-element.73.refs_0_, f32[2,64,384]{2,1,0:T(8,128)S(1)} %collective-permute-done.4.refs_1_, f32[2,64,384]{2,1,0:T(8,128)S(1)} %collective-permute-done.5.refs_2_, f32[2,64,384]{2,1,0:T(8,128)S(1)} %collective-permute-done.6.refs_3_, ...), custom_call_target="tpu_custom_call", output_to_operand_aliasing={{}: (8, {})} | custom-call | flops 603979776 | bytes 1572864 | tf_op jit(solution)/shard_map/z_step/pallas_call | solution.py:310
  (39 shorter events, 0.2 us)
Async XLA Ops:
  0.0 4.4 %collective-permute-start = (f32[2,1024,256]{2,1,0:T(8,128)}, f32[2,1024,256]{2,1,0:T(8,128)S(1)}, u32[]{:S(2)}, u32[]{:S(2)}) collective-permute-start(f32[2,1024,256]{2,1,0:T(8,128)} %bitcast.3), channel_id=1, source_target_pairs={{0,4},{4,0},{8,12},{12,8},{16,20},{20,16},{24,28},{28,24},{1,5},{5... | collective-permute-start | bytes 6291464 | tf_op jit(solution)/shard_map/ppermute | solution.py:261
  0.0 1.6 %copy-start.1 = (f32[2,256,32,32]{1,3,2,0:T(8,128)S(1)}, f32[2,256,32,32]{1,3,2,0:T(8,128)}, u32[]{:S(2)}) copy-start(f32[2,256,32,32]{1,3,2,0:T(8,128)} %param.9) | copy-start | bytes 6291460
  1.6 0.9 %copy-start.2 = (bf16[512,256]{1,0:T(8,128)(2,1)S(1)}, bf16[512,256]{1,0:T(8,128)(2,1)}, u32[]{:S(2)}) copy-start(bf16[512,256]{1,0:T(8,128)(2,1)} %constant.27.clone.table_ref) | copy-start | bytes 786436
  2.5 1.8 %copy-start.3 = (bf16[512,256]{1,0:T(8,128)(2,1)S(1)}, bf16[512,256]{1,0:T(8,128)(2,1)}, u32[]{:S(2)}) copy-start(bf16[512,256]{1,0:T(8,128)(2,1)} %constant.27.clone.table_ref) | copy-start | bytes 786436
  4.4 22.7 %copy-start = (bf16[256,768]{1,0:T(8,128)(2,1)S(1)}, bf16[256,768]{1,0:T(8,128)(2,1)}, u32[]{:S(2)}) copy-start(bf16[256,768]{1,0:T(8,128)(2,1)} %constant.28.clone.refs_4_) | copy-start | bytes 1179652
  5.5 39.4 %copy-start.7 = (f32[256]{0:T(256)S(1)}, f32[256]{0:T(256)}, u32[]{:S(2)}) copy-start(f32[256]{0:T(256)} %param.12) | copy-start | bytes 3076
  5.5 64.0 %copy-start.6 = (f32[128]{0:T(128)S(1)}, f32[128]{0:T(128)}, u32[]{:S(2)}) copy-start(f32[128]{0:T(128)} %param.13) | copy-start | bytes 1540
  5.5 64.0 %copy-start.8 = (f32[2,2]{1,0:T(2,128)S(1)}, f32[2,2]{1,0:T(2,128)}, u32[]{:S(2)}) copy-start(f32[2,2]{1,0:T(2,128)} %param.10) | copy-start | bytes 52
  5.6 64.1 %copy-start.9 = (f32[256]{0:T(256)S(1)}, f32[256]{0:T(256)}, u32[]{:S(2)}) copy-start(f32[256]{0:T(256)} %param.11) | copy-start | bytes 3076
  5.6 64.2 %copy-start.4 = (bf16[128,128]{1,0:T(8,128)(2,1)S(1)}, bf16[128,128]{1,0:T(8,128)(2,1)}, u32[]{:S(2)}) copy-start(bf16[128,128]{1,0:T(8,128)(2,1)} %constant.29.clone.table_high) | copy-start | bytes 98308
  5.6 64.2 %copy-start.5 = (bf16[128,128]{1,0:T(8,128)(2,1)S(1)}, bf16[128,128]{1,0:T(8,128)(2,1)}, u32[]{:S(2)}) copy-start(bf16[128,128]{1,0:T(8,128)(2,1)} %constant.30.clone.table_low) | copy-start | bytes 98308
  5.6 6.6 %collective-permute-start.19 = (f32[2,64,128]{2,1,0:T(8,128)S(1)}, f32[2,64,128]{2,1,0:T(8,128)S(1)}, u32[]{:S(2)}, u32[]{:S(2)}) collective-permute-start(f32[2,64,128]{2,1,0:T(8,128)S(1)} %get-tuple-element.94), channel_id=1, source_target_pairs={{0,8},{4,12},{8,0},{12,4},{16,24},{20,28},{24,16},{28,20},{1,9},{5... | collective-permute-start | bytes 196616 | tf_op jit(solution)/shard_map/ppermute | solution.py:203
  7.2 5.5 %collective-permute-start.20 = (f32[2,64,128]{2,1,0:T(8,128)S(1)}, f32[2,64,128]{2,1,0:T(8,128)S(1)}, u32[]{:S(2)}, u32[]{:S(2)}) collective-permute-start(f32[2,64,128]{2,1,0:T(8,128)S(1)} %get-tuple-element.95), channel_id=1, source_target_pairs={{0,16},{4,20},{8,24},{12,28},{16,0},{20,4},{24,8},{28,12},{1,17},{... | collective-permute-start | bytes 196616 | tf_op jit(solution)/shard_map/ppermute | solution.py:203
  8.7 13.5 %collective-permute-start.7 = (f32[2,64,256]{2,1,0:T(8,128)S(1)}, f32[2,64,256]{2,1,0:T(8,128)S(1)}, u32[]{:S(2)}, u32[]{:S(2)}) collective-permute-start(f32[2,64,256]{2,1,0:T(8,128)S(1)} %get-tuple-element.78), channel_id=1, source_target_pairs={{0,8},{4,12},{8,0},{12,4},{16,24},{20,28},{24,16},{28,20},{1,9},{5... | collective-permute-start | bytes 393224 | tf_op jit(solution)/shard_map/ppermute | solution.py:203
  9.2 14.4 %collective-permute-start.8 = (f32[2,64,256]{2,1,0:T(8,128)S(1)}, f32[2,64,256]{2,1,0:T(8,128)S(1)}, u32[]{:S(2)}, u32[]{:S(2)}) collective-permute-start(f32[2,64,256]{2,1,0:T(8,128)S(1)} %get-tuple-element.79), channel_id=1, source_target_pairs={{0,16},{4,20},{8,24},{12,28},{16,0},{20,4},{24,8},{28,12},{1,17},{... | collective-permute-start | bytes 393224 | tf_op jit(solution)/shard_map/ppermute | solution.py:203
  9.7 14.5 %collective-permute-start.9 = (f32[2,64,256]{2,1,0:T(8,128)S(1)}, f32[2,64,256]{2,1,0:T(8,128)S(1)}, u32[]{:S(2)}, u32[]{:S(2)}) collective-permute-start(f32[2,64,256]{2,1,0:T(8,128)S(1)} %get-tuple-element.80), channel_id=1, source_target_pairs={{0,24},{4,28},{8,16},{12,20},{16,8},{20,12},{24,0},{28,4},{1,25},{... | collective-permute-start | bytes 393224 | tf_op jit(solution)/shard_map/ppermute | solution.py:203
  12.2 13.5 %collective-permute-start.13 = (f32[2,64,256]{2,1,0:T(8,128)S(1)}, f32[2,64,256]{2,1,0:T(8,128)S(1)}, u32[]{:S(2)}, u32[]{:S(2)}) collective-permute-start(f32[2,64,256]{2,1,0:T(8,128)S(1)} %get-tuple-element.86), channel_id=1, source_target_pairs={{0,8},{4,12},{8,0},{12,4},{16,24},{20,28},{24,16},{28,20},{1,9},{5... | collective-permute-start | bytes 393224 | tf_op jit(solution)/shard_map/ppermute | solution.py:203
  12.7 8.0 %collective-permute-start.21 = (f32[2,64,128]{2,1,0:T(8,128)S(1)}, f32[2,64,128]{2,1,0:T(8,128)S(1)}, u32[]{:S(2)}, u32[]{:S(2)}) collective-permute-start(f32[2,64,128]{2,1,0:T(8,128)S(1)} %get-tuple-element.96), channel_id=1, source_target_pairs={{0,24},{4,28},{8,16},{12,20},{16,8},{20,12},{24,0},{28,4},{1,25},{... | collective-permute-start | bytes 196616 | tf_op jit(solution)/shard_map/ppermute | solution.py:203
  20.7 10.0 %collective-permute-start.14 = (f32[2,64,256]{2,1,0:T(8,128)S(1)}, f32[2,64,256]{2,1,0:T(8,128)S(1)}, u32[]{:S(2)}, u32[]{:S(2)}) collective-permute-start(f32[2,64,256]{2,1,0:T(8,128)S(1)} %get-tuple-element.87), channel_id=1, source_target_pairs={{0,16},{4,20},{8,24},{12,28},{16,0},{20,4},{24,8},{28,12},{1,17},{... | collective-permute-start | bytes 393224 | tf_op jit(solution)/shard_map/ppermute | solution.py:203
  22.1 10.1 %collective-permute-start.15 = (f32[2,64,256]{2,1,0:T(8,128)S(1)}, f32[2,64,256]{2,1,0:T(8,128)S(1)}, u32[]{:S(2)}, u32[]{:S(2)}) collective-permute-start(f32[2,64,256]{2,1,0:T(8,128)S(1)} %get-tuple-element.88), channel_id=1, source_target_pairs={{0,24},{4,28},{8,16},{12,20},{16,8},{20,12},{24,0},{28,4},{1,25},{... | collective-permute-start | bytes 393224 | tf_op jit(solution)/shard_map/ppermute | solution.py:203
  23.6 19.2 %collective-permute-start.1 = (f32[2,64,384]{2,1,0:T(8,128)S(1)}, f32[2,64,384]{2,1,0:T(8,128)S(1)}, u32[]{:S(2)}, u32[]{:S(2)}) collective-permute-start(f32[2,64,384]{2,1,0:T(8,128)S(1)} %get-tuple-element.70), channel_id=1, source_target_pairs={{0,8},{4,12},{8,0},{12,4},{16,24},{20,28},{24,16},{28,20},{1,9},{5... | collective-permute-start | bytes 589832 | tf_op jit(solution)/shard_map/ppermute | solution.py:203
  24.2 18.6 %collective-permute-start.2 = (f32[2,64,384]{2,1,0:T(8,128)S(1)}, f32[2,64,384]{2,1,0:T(8,128)S(1)}, u32[]{:S(2)}, u32[]{:S(2)}) collective-permute-start(f32[2,64,384]{2,1,0:T(8,128)S(1)} %get-tuple-element.71), channel_id=1, source_target_pairs={{0,16},{4,20},{8,24},{12,28},{16,0},{20,4},{24,8},{28,12},{1,17},{... | collective-permute-start | bytes 589832 | tf_op jit(solution)/shard_map/ppermute | solution.py:203
  25.6 18.6 %collective-permute-start.3 = (f32[2,64,384]{2,1,0:T(8,128)S(1)}, f32[2,64,384]{2,1,0:T(8,128)S(1)}, u32[]{:S(2)}, u32[]{:S(2)}) collective-permute-start(f32[2,64,384]{2,1,0:T(8,128)S(1)} %get-tuple-element.72), channel_id=1, source_target_pairs={{0,24},{4,28},{8,16},{12,20},{16,8},{20,12},{24,0},{28,4},{1,25},{... | collective-permute-start | bytes 589832 | tf_op jit(solution)/shard_map/ppermute | solution.py:203
  30.7 5.0 %collective-permute-start.22 = (f32[2,64,128]{2,1,0:T(8,128)S(1)}, f32[2,64,128]{2,1,0:T(8,128)S(1)}, u32[]{:S(2)}, u32[]{:S(2)}) collective-permute-start(f32[2,64,128]{2,1,0:T(8,128)S(1)} %get-tuple-element.98), channel_id=1, source_target_pairs={{0,1},{1,0},{2,3},{3,2},{4,5},{5,4},{6,7},{7,6},{8,9},{9,8},{10,11... | collective-permute-start | bytes 196616 | tf_op jit(solution)/shard_map/ppermute | solution.py:203
  32.3 6.9 %collective-permute-start.23 = (f32[2,64,128]{2,1,0:T(8,128)S(1)}, f32[2,64,128]{2,1,0:T(8,128)S(1)}, u32[]{:S(2)}, u32[]{:S(2)}) collective-permute-start(f32[2,64,128]{2,1,0:T(8,128)S(1)} %get-tuple-element.99), channel_id=1, source_target_pairs={{0,2},{1,3},{2,0},{3,1},{4,6},{5,7},{6,4},{7,5},{8,10},{9,11},{10,... | collective-permute-start | bytes 196616 | tf_op jit(solution)/shard_map/ppermute | solution.py:203
  35.7 27.9 %collective-permute-start.10 = (f32[2,64,256]{2,1,0:T(8,128)}, f32[2,64,256]{2,1,0:T(8,128)S(1)}, u32[]{:S(2)}, u32[]{:S(2)}) collective-permute-start(f32[2,64,256]{2,1,0:T(8,128)} %get-tuple-element.82), channel_id=1, source_target_pairs={{0,1},{1,0},{2,3},{3,2},{4,5},{5,4},{6,7},{7,6},{8,9},{9,8},{10,11... | collective-permute-start | bytes 393224 | tf_op jit(solution)/shard_map/ppermute | solution.py:203
  39.2 25.0 %collective-permute-start.16 = (f32[2,64,256]{2,1,0:T(8,128)}, f32[2,64,256]{2,1,0:T(8,128)S(1)}, u32[]{:S(2)}, u32[]{:S(2)}) collective-permute-start(f32[2,64,256]{2,1,0:T(8,128)} %get-tuple-element.90), channel_id=1, source_target_pairs={{0,1},{1,0},{2,3},{3,2},{4,5},{5,4},{6,7},{7,6},{8,9},{9,8},{10,11... | collective-permute-start | bytes 393224 | tf_op jit(solution)/shard_map/ppermute | solution.py:203
  42.8 25.2 %collective-permute-start.17 = (f32[2,64,256]{2,1,0:T(8,128)}, f32[2,64,256]{2,1,0:T(8,128)S(1)}, u32[]{:S(2)}, u32[]{:S(2)}) collective-permute-start(f32[2,64,256]{2,1,0:T(8,128)} %get-tuple-element.91), channel_id=1, source_target_pairs={{0,2},{1,3},{2,0},{3,1},{4,6},{5,7},{6,4},{7,5},{8,10},{9,11},{10,... | collective-permute-start | bytes 393224 | tf_op jit(solution)/shard_map/ppermute | solution.py:203
  42.8 25.3 %collective-permute-start.18 = (f32[2,64,256]{2,1,0:T(8,128)S(1)}, f32[2,64,256]{2,1,0:T(8,128)S(1)}, u32[]{:S(2)}, u32[]{:S(2)}) collective-permute-start(f32[2,64,256]{2,1,0:T(8,128)S(1)} %get-tuple-element.92), channel_id=1, source_target_pairs={{0,3},{1,2},{2,1},{3,0},{4,7},{5,6},{6,5},{7,4},{8,11},{9,10},{10,... | collective-permute-start | bytes 393224 | tf_op jit(solution)/shard_map/ppermute | solution.py:203
  44.3 19.3 %collective-permute-start.24 = (f32[2,64,128]{2,1,0:T(8,128)S(1)}, f32[2,64,128]{2,1,0:T(8,128)S(1)}, u32[]{:S(2)}, u32[]{:S(2)}) collective-permute-start(f32[2,64,128]{2,1,0:T(8,128)S(1)} %get-tuple-element.100), channel_id=1, source_target_pairs={{0,3},{1,2},{2,1},{3,0},{4,7},{5,6},{6,5},{7,4},{8,11},{9,10},{10,... | collective-permute-start | bytes 196616 | tf_op jit(solution)/shard_map/ppermute | solution.py:203
  63.6 9.0 %collective-permute-start.11 = (f32[2,64,256]{2,1,0:T(8,128)S(1)}, f32[2,64,256]{2,1,0:T(8,128)S(1)}, u32[]{:S(2)}, u32[]{:S(2)}) collective-permute-start(f32[2,64,256]{2,1,0:T(8,128)S(1)} %get-tuple-element.83), channel_id=1, source_target_pairs={{0,2},{1,3},{2,0},{3,1},{4,6},{5,7},{6,4},{7,5},{8,10},{9,11},{10,... | collective-permute-start | bytes 393224 | tf_op jit(solution)/shard_map/ppermute | solution.py:203
  63.6 9.0 %collective-permute-start.12 = (f32[2,64,256]{2,1,0:T(8,128)S(1)}, f32[2,64,256]{2,1,0:T(8,128)S(1)}, u32[]{:S(2)}, u32[]{:S(2)}) collective-permute-start(f32[2,64,256]{2,1,0:T(8,128)S(1)} %get-tuple-element.84), channel_id=1, source_target_pairs={{0,3},{1,2},{2,1},{3,0},{4,7},{5,6},{6,5},{7,4},{8,11},{9,10},{10,... | collective-permute-start | bytes 393224 | tf_op jit(solution)/shard_map/ppermute | solution.py:203
  64.2 9.8 %collective-permute-start.4 = (f32[2,64,384]{2,1,0:T(8,128)S(1)}, f32[2,64,384]{2,1,0:T(8,128)S(1)}, u32[]{:S(2)}, u32[]{:S(2)}) collective-permute-start(f32[2,64,384]{2,1,0:T(8,128)S(1)} %get-tuple-element.74), channel_id=1, source_target_pairs={{0,1},{1,0},{2,3},{3,2},{4,5},{5,4},{6,7},{7,6},{8,9},{9,8},{10,11... | collective-permute-start | bytes 589832 | tf_op jit(solution)/shard_map/ppermute | solution.py:203
  68.0 8.7 %collective-permute-start.5 = (f32[2,64,384]{2,1,0:T(8,128)S(1)}, f32[2,64,384]{2,1,0:T(8,128)S(1)}, u32[]{:S(2)}, u32[]{:S(2)}) collective-permute-start(f32[2,64,384]{2,1,0:T(8,128)S(1)} %get-tuple-element.75), channel_id=1, source_target_pairs={{0,2},{1,3},{2,0},{3,1},{4,6},{5,7},{6,4},{7,5},{8,10},{9,11},{10,... | collective-permute-start | bytes 589832 | tf_op jit(solution)/shard_map/ppermute | solution.py:203
  68.1 11.7 %collective-permute-start.6 = (f32[2,64,384]{2,1,0:T(8,128)S(1)}, f32[2,64,384]{2,1,0:T(8,128)S(1)}, u32[]{:S(2)}, u32[]{:S(2)}) collective-permute-start(f32[2,64,384]{2,1,0:T(8,128)S(1)} %get-tuple-element.76), channel_id=1, source_target_pairs={{0,3},{1,2},{2,1},{3,0},{4,7},{5,6},{6,5},{7,4},{8,11},{9,10},{10,... | collective-permute-start | bytes 589832 | tf_op jit(solution)/shard_map/ppermute | solution.py:203
